TPU v7x, 32 devices: a whole 2x2x4 slice. The times are simulated.
32 devices in a mesh: dp: 2 (over core), gx: 4 (over y, x), gy: 4 (over z).
Axes of the slice: x: 2, y: 2, z: 4, core: 2. Of those that a mesh axis runs over, the one named last changes fastest.
Arguments:
- volume: bfloat16 [2, 4, 8, 32, 128], P('dp', None, 'gx', 'gy'), may hold values from -6 to 6
- targets: float32 [2, 4], P('dp'), may hold values from -4 to 4
- conv1_w: bfloat16 [27, 128], replicated, may hold values from -0.625 to 0.625
- conv1_b: float32 [32], replicated, may hold values from -3 to 3
- conv2_w: bfloat16 [27, 2048], replicated, may hold values from -0.21875 to 0.21875
- conv2_b: float32 [64], replicated, may hold values from -3 to 3
- head_w: float32 [64, 4], replicated, may hold values from -2 to 2
- head_b: float32 [4], replicated, may hold values from -4 to 4
- dir1: float32 [27, 128], replicated, may hold values from -6 to 6
- dir2: float32 [27, 2048], replicated, may hold values from -1.2 to 1.2
- dir_head: float32 [64, 4], replicated, may hold values from -6 to 6
Outputs:
- next1: float32 [27, 128], replicated
- next2: float32 [27, 2048], replicated
- next_head: float32 [64, 4], replicated
- rayleigh: float32 [], replicated
- curvature_field: float32 [2, 32, 8, 32, 128], P('dp', None, 'gx', 'gy')
All inputs are finite; a program needn't handle non-finite values.
Results may differ from a plain program's by a relative error of at most 0.0051.
Values may be sent and summed in bfloat16 or wider, within the bound.
A program may use at most 128 MiB of HBM per device.

v0:
```python
import jax
import jax.numpy as jnp
from jax import lax
from jax.sharding import PartitionSpec as P

C0 = 4
C1 = 32
C2 = 64


def extended(cells, sides, width):
    for axis, dim in sides:
        count = lax.axis_size(axis)
        ends = count - 1
        head = lax.slice_in_dim(cells, 0, width, axis=dim)
        tail = lax.slice_in_dim(cells, cells.shape[dim] - width, cells.shape[dim], axis=dim)
        cells = jnp.concatenate(
            [
                lax.ppermute(tail, axis, [(i, (i + 1) % count) for i in range(ends)]),
                cells,
                lax.ppermute(head, axis, [((i + 1) % count, i) for i in range(ends)]),
            ],
            axis=dim,
        )
    return cells


def silu_parts(z):
    s = jax.nn.sigmoid(z)
    return (z * s, s * (1.0 + z * (1.0 - s)), s * (1.0 - s) * (2.0 + z * (1.0 - 2.0 * s)))


def as_kernel(flat, outer, inner):
    return flat.reshape(3, 3, 3, outer, inner).transpose(3, 4, 0, 1, 2)


def pad_depth(a):
    return jnp.pad(a, ((0, 0), (0, 0), (0, 0), (0, 0), (1, 1)))


def convolve(padded, kernel):
    return lax.conv_general_dilated(
        pad_depth(padded),
        kernel,
        (1, 1, 1),
        "VALID",
        dimension_numbers=("NCDHW", "OIDHW", "NCDHW"),
        preferred_element_type=jnp.float32,
    )


def flipped(kernel):
    return jnp.flip(kernel, (2, 3, 4)).transpose(1, 0, 2, 3, 4)


def correlate(padded, grads):
    wide = pad_depth(padded)
    sx, sy, sz = (grads.shape[2], grads.shape[3], grads.shape[4])
    pieces = []
    for a in range(3):
        for b in range(3):
            for c in range(3):
                window = wide[:, :, a : a + sx, b : b + sy, c : c + sz]
                pieces.append(
                    jnp.einsum("bixyz,boxyz->oi", window, grads, preferred_element_type=jnp.float32)
                )
    stacked = jnp.stack(pieces, axis=0)
    return stacked.reshape(27, grads.shape[1] * padded.shape[1])


def spread(vector):
    return vector[:, :, None, None, None]


def per_device(
    volume, targets, conv1_w, conv1_b, conv2_w, conv2_b, head_w, head_b, dir1, dir2, dir_head
):
    high = lax.Precision.HIGHEST
    weight1 = as_kernel(conv1_w, C1, C0)
    weight2 = as_kernel(conv2_w, C2, C1)
    kern1 = as_kernel(dir1.astype(jnp.bfloat16), C1, C0)
    kern2 = as_kernel(dir2.astype(jnp.bfloat16), C2, C1)
    depth, height = (volume.shape[2], volume.shape[3])
    padded_in = extended(volume, (("gx", 2), ("gy", 3)), 1)
    z1 = convolve(padded_in, weight1) + conv1_b[None, :, None, None, None]
    t1 = convolve(padded_in, kern1)
    act1, slope1, bend1 = silu_parts(z1)
    a1 = act1.astype(jnp.bfloat16)
    ta1 = (slope1 * t1).astype(jnp.bfloat16)
    pa1 = extended(a1, (("gx", 2), ("gy", 3)), 1)
    pta1 = extended(ta1, (("gx", 2), ("gy", 3)), 1)
    z2 = convolve(pa1, weight2) + conv2_b[None, :, None, None, None]
    t2 = convolve(pta1, weight2) + convolve(pa1, kern2)
    act2, slope2, bend2 = silu_parts(z2)
    width = z2.shape[4]
    cells = depth * lax.axis_size("gx") * height * lax.axis_size("gy") * width
    sums = lax.psum(
        (jnp.sum(act2, axis=(2, 3, 4)), jnp.sum(slope2 * t2, axis=(2, 3, 4))), ("gx", "gy")
    )
    pooled = sums[0] / cells
    tpooled = sums[1] / cells
    batch = volume.shape[0] * lax.axis_size("dp")
    outputs = jnp.dot(pooled, head_w, precision=high) + head_b
    toutputs = jnp.dot(tpooled, head_w, precision=high) + jnp.dot(pooled, dir_head, precision=high)
    dy = (outputs - targets) / batch
    tdy = toutputs / batch
    leader = ((lax.axis_index("gx") == 0) & (lax.axis_index("gy") == 0)).astype(jnp.float32)
    hd = leader * (jnp.dot(tpooled.T, dy, precision=high) + jnp.dot(pooled.T, tdy, precision=high))
    dpool = jnp.dot(dy, head_w.T, precision=high) / cells
    tdpool = (
        jnp.dot(tdy, head_w.T, precision=high) + jnp.dot(dy, dir_head.T, precision=high)
    ) / cells
    g2 = (slope2 * spread(dpool)).astype(jnp.bfloat16)
    tg2 = (bend2 * t2 * spread(dpool) + slope2 * spread(tdpool)).astype(jnp.bfloat16)
    back_w = flipped(weight2)
    back_k = flipped(kern2)
    joined = extended(jnp.stack((g2, tg2)), (("gx", 3), ("gy", 4)), 1)
    pg2, ptg2 = (joined[0], joined[1])
    da1 = convolve(pg2, back_w)
    tda1 = convolve(ptg2, back_w) + convolve(pg2, back_k)
    tg1 = (bend1 * t1 * da1 + slope1 * tda1).astype(jnp.bfloat16)
    h1 = correlate(padded_in, tg1)
    h2 = correlate(pa1, tg2) + correlate(pta1, g2)
    h1, h2, hd = lax.psum((h1, h2, hd), ("dp", "gx", "gy"))
    field = tda1 * cells
    quad = jnp.sum(dir1 * h1) + jnp.sum(dir2 * h2) + jnp.sum(dir_head * hd)
    length = jnp.sum(dir1 * dir1) + jnp.sum(dir2 * dir2) + jnp.sum(dir_head * dir_head)
    nrm = jnp.sqrt(jnp.sum(h1 * h1) + jnp.sum(h2 * h2) + jnp.sum(hd * hd) + 1e-06)
    return (h1 / nrm, h2 / nrm, hd / nrm, quad / length, field)


def solution(mesh):
    return jax.shard_map(
        per_device,
        mesh=mesh,
        in_specs=(
            P("dp", None, "gx", "gy", None),
            P("dp", None),
            P(),
            P(),
            P(),
            P(),
            P(),
            P(),
            P(),
            P(),
            P(),
        ),
        out_specs=(P(), P(), P(), P(), P("dp", None, "gx", "gy", None)),
        check_vma=False,
    )
```

profile of v0, /device:TPU:0, one launch (start us, length us, event | category | flops | bytes accessed | tf_op | source)
XLA Modules:
  0.0 376.5 jit_solution(5744117732220031743)
XLA Ops:
  8.0 4.9 %collective-permute-start = (bf16[1,4,1,8,128]{4,1,3,2,0:T(4,128)(2,1)S(1)}, bf16[1,4,1,8,128]{4,1,3,2,0:T(4,128)(2,1)S(1)}, u32[]{:S(2)}, u32[]{:S(2)}) collective-permute-start(bf16[1,4,1,8,128]{4,1,3,2,0:T(4,128)(2,1)S(1)} %get-tuple-element.60), channel_id=1, source_target_pairs={{0,4},{4,8},{8,12},{1,5},{5,9},{9,13},{2,6},{6,10},{10,14},{3,7},{... | collective-permute-start | bytes 24584 | tf_op jit(solution)/shard_map/ppermute | solution.py:19
  12.9 1.3 collective-permute-start.1
  15.0 3.5 collective-permute-done.1
  18.5 1.3 collective-permute-start.3
  19.8 4.5 %collective-permute-start.2 = (bf16[1,4,4,1,128]{4,1,3,2,0:T(4,128)(2,1)S(1)}, bf16[1,4,4,1,128]{4,1,3,2,0:T(4,128)(2,1)S(1)}, u32[]{:S(2)}, u32[]{:S(2)}) collective-permute-start(bf16[1,4,4,1,128]{4,1,3,2,0:T(4,128)(2,1)S(1)} %get-tuple-element.57), channel_id=1, source_target_pairs={{0,1},{1,2},{2,3},{4,5},{5,6},{6,7},{8,9},{9,10},{10,11},{12,13},{... | collective-permute-start | bytes 12296 | tf_op jit(solution)/shard_map/ppermute | solution.py:19
  24.3 2.0 reshape.567
  26.3 1.2 reshape.565
  28.8 1.1 reshape.570
  30.4 1.4 copy.299
  31.9 6.4 %fusion.38 = f32[2,8,8,17,32]{4,2,3,1,0:T(8,128)S(1)} fusion(bf16[3,3,3,32,4]{4,3,2,1,0:T(8,128)(2,1)S(1)} %reshape.565, f32[32]{0:T(128)S(1)} %copy-done.53, pred[8,17]{0,1:T(8,128)(4,1)S(1)} %copy-done.57, bf16[4,4,10,1,7,2]{4,0,5,2,1,3:T(4,128)(2,1)S(1)} %slice.473, bf16[4,4,10,1,8,17]{4,0,5,2,1,3:T(4,128)(2,1)S(1)} %copy.299), kind=kOutput, calls=%fused_computation.77 | convolution fusion | flops 15325696 | bytes 333704 | tf_op jit(solution)/shard_map/conv_general_dilated | solution.py:42
  38.3 7.7 %multiply_convert_fusion.1 = (bf16[2,8,8,17,32]{4,2,3,1,0:T(8,128)(2,1)S(1)}, bf16[2,8,8,17,32]{4,2,3,1,0:T(8,128)(2,1)S(1)}, f32[2,8,8,17,32]{4,2,3,1,0:T(8,128)}) fusion(f32[2,8,8,17,32]{4,2,3,1,0:T(8,128)S(1)} %fusion.38, bf16[3,3,3,32,4]{4,3,2,1,0:T(8,128)(2,1)S(1)} %reshape.566, bf16[4,4,10,1,7,2]{4,0,5,2,1,3:T(4,128)(2,1)S(1)} %slice.473, ...), kind=kOutput, calls=%fused_computation.95 | convolution fusion | flops 16022016 | bytes 890632 | tf_op jit(solution)/shard_map/conv_general_dilated | solution.py:42
  46.5 1.3 collective-permute-start.5
  48.4 4.9 %collective-permute-start.4 = (bf16[1,32,1,8,128]{4,1,3,2,0:T(8,128)(2,1)S(1)}, bf16[1,32,1,8,128]{4,1,3,2,0:T(8,128)(2,1)S(1)}, u32[]{:S(2)}, u32[]{:S(2)}) collective-permute-start(bf16[1,32,1,8,128]{4,1,3,2,0:T(8,128)(2,1)S(1)} %bitcast.755), channel_id=1, source_target_pairs={{0,4},{4,8},{8,12},{1,5},{5,9},{9,13},{2,6},{6,10},{10,14},{3,7},{... | collective-permute-start | bytes 196616 | tf_op jit(solution)/shard_map/ppermute | solution.py:19
  53.6 1.3 collective-permute-start.9
  55.6 5.4 %collective-permute-start.8 = (bf16[1,32,1,8,128]{4,1,3,2,0:T(8,128)(2,1)S(1)}, bf16[1,32,1,8,128]{4,1,3,2,0:T(8,128)(2,1)S(1)}, u32[]{:S(2)}, u32[]{:S(2)}) collective-permute-start(bf16[1,32,1,8,128]{4,1,3,2,0:T(8,128)(2,1)S(1)} %bitcast.756), channel_id=1, source_target_pairs={{0,4},{4,8},{8,12},{1,5},{5,9},{9,13},{2,6},{6,10},{10,14},{3,7},{... | collective-permute-start | bytes 196616 | tf_op jit(solution)/shard_map/ppermute | solution.py:19
  61.2 1.3 collective-permute-start.7
  62.5 4.5 %collective-permute-start.6 = (bf16[1,32,4,1,128]{4,1,3,2,0:T(8,128)(2,1)S(1)}, bf16[1,32,4,1,128]{4,1,3,2,0:T(8,128)(2,1)S(1)}, u32[]{:S(2)}, u32[]{:S(2)}) collective-permute-start(bf16[1,32,4,1,128]{4,1,3,2,0:T(8,128)(2,1)S(1)} %get-tuple-element.55), channel_id=1, source_target_pairs={{0,1},{1,2},{2,3},{4,5},{5,6},{6,7},{8,9},{9,10},{10,11},{12,13},{... | collective-permute-start | bytes 98312 | tf_op jit(solution)/shard_map/ppermute | solution.py:19
  67.7 1.3 collective-permute-start.11
  69.0 4.5 %collective-permute-start.10 = (bf16[1,32,4,1,128]{4,1,3,2,0:T(8,128)(2,1)}, bf16[1,32,4,1,128]{4,1,3,2,0:T(8,128)(2,1)S(1)}, u32[]{:S(2)}, u32[]{:S(2)}) collective-permute-start(bf16[1,32,4,1,128]{4,1,3,2,0:T(8,128)(2,1)} %get-tuple-element.53), channel_id=1, source_target_pairs={{0,1},{1,2},{2,3},{4,5},{5,6},{6,7},{8,9},{9,10},{10,11},{12,13},{... | collective-permute-start | bytes 98312 | tf_op jit(solution)/shard_map/ppermute | solution.py:19
  78.7 1.9 convolution_select_fusion.2
  80.7 1.9 fusion.37
  82.7 2.4 select_reduce_fusion
  85.1 39.3 %all-reduce.4 = (f32[1,64]{1,0:T(1,128)S(1)}, f32[1,64]{1,0:T(1,128)S(1)}) all-reduce(f32[1,64]{1,0:T(1,128)S(1)} %bitcast.760, f32[1,64]{1,0:T(1,128)S(1)} %bitcast.759), channel_id=1, replica_groups=mesh['dp'=2,'gx'=4,'gy'=4] {'gx','gy'}, use_global_device_ids=true, to_apply=%region_1.2 | all-reduce | flops 128 | bytes 1024 | tf_op jit(solution)/shard_map/psum | solution.py:97
  126.2 2.1 multiply_convert_fusion
  131.4 0.8 convolution_bitcast_fusion.52
  132.2 0.8 convolution_bitcast_fusion.43
  134.4 0.8 convolution_bitcast_fusion.46
  135.2 0.8 convolution_bitcast_fusion.37
  136.6 0.8 convolution_bitcast_fusion.34
  138.6 0.8 convolution_bitcast_fusion.28
  142.8 0.8 convolution_bitcast_fusion.25
  143.6 0.8 convolution_bitcast_fusion.16
  145.8 0.8 convolution_bitcast_fusion.19
  146.6 0.8 convolution_bitcast_fusion.10
  149.7 1.3 collective-permute-start.13
  151.0 4.6 %collective-permute-start.12 = (bf16[2,1,64,1,8,128]{5,2,4,3,1,0:T(8,128)(2,1)S(1)}, bf16[2,1,64,1,8,128]{5,2,4,3,1,0:T(8,128)(2,1)S(1)}, u32[]{:S(2)}, u32[]{:S(2)}) collective-permute-start(bf16[2,1,64,1,8,128]{5,2,4,3,1,0:T(8,128)(2,1)S(1)} %get-tuple-element.47), channel_id=1, source_target_pairs={{0,4},{4,8},{8,12},{1,5},{5,9},{9,13},{2,6},{6,10},{10,14},{3,7},{... | collective-permute-start | bytes 786440 | tf_op jit(solution)/shard_map/ppermute | solution.py:19
  156.8 0.8 stack.293
  163.9 1.3 collective-permute-start.15
  165.2 4.6 %collective-permute-start.14 = (bf16[2,1,64,4,1,128]{5,2,4,3,1,0:T(8,128)(2,1)S(1)}, bf16[2,1,64,4,1,128]{5,2,4,3,1,0:T(8,128)(2,1)S(1)}, u32[]{:S(2)}, u32[]{:S(2)}) collective-permute-start(bf16[2,1,64,4,1,128]{5,2,4,3,1,0:T(8,128)(2,1)S(1)} %get-tuple-element.41), channel_id=1, source_target_pairs={{0,1},{1,2},{2,3},{4,5},{5,6},{6,7},{8,9},{9,10},{10,11},{12,13},{... | collective-permute-start | bytes 393224 | tf_op jit(solution)/shard_map/ppermute | solution.py:19
  169.7 121.5 %all-reduce.7.cloned.1.call-done = f32[27,2048]{1,0:T(8,128)} async-done(((f32[27,2048]{1,0:T(8,128)}), f32[27,2048]{1,0:T(8,128)}) %all-reduce.7.cloned.1.call-update) | async-done | bytes 221200 | tf_op jit(solution)/shard_map/psum | solution.py:124
  291.3 1.7 multiply_reduce_fusion
  293.4 1.6 copy.591
  296.7 3.3 convolution_select_fusion
  300.0 1.8 copy.592
  303.9 2.4 broadcast_multiply_fusion
  306.3 2.7 fusion.39
  318.4 39.5 %all-reduce.3 = (f32[27,128]{1,0:T(8,128)S(1)}, f32[64,4]{0,1:T(4,128)S(1)}) all-reduce(f32[27,128]{1,0:T(8,128)S(1)} %stack.291, f32[64,4]{0,1:T(4,128)S(1)} %add_multiply_fusion), channel_id=1, replica_groups=mesh['dp'=2,'gx'=4,'gy'=4] {'dp','gx','gy'}, use_global_device_ids=true, to_apply=%region_4.5 | all-reduce | flops 3712 | bytes 29696 | tf_op jit(solution)/shard_map/psum | solution.py:124
  362.6 1.1 copy.415
  (384 shorter events, 49.6 us)
Async XLA Ops:
  7.2 117.2 %copy-start = (f32[64,4]{0,1:T(4,128)S(1)}, f32[64,4]{0,1:T(4,128)}, u32[]{:S(2)}) copy-start(f32[64,4]{0,1:T(4,128)} %param.17) | copy-start | bytes 3076
  7.2 21.5 %copy-start.13 = (f32[27,2048]{1,0:T(8,128)S(1)}, f32[27,2048]{1,0:T(8,128)}, u32[]{:S(2)}) copy-start(f32[27,2048]{1,0:T(8,128)} %param.20) | copy-start | bytes 663556
  7.2 284.1 %all-reduce.7.cloned.1.call-start = ((), (), s32[]{:S(2)}) async-start(), calls=%async_computation | async-start | bytes 524288 | tf_op jit(solution)/shard_map/psum | solution.py:124
  8.0 6.2 %collective-permute-start = (bf16[1,4,1,8,128]{4,1,3,2,0:T(4,128)(2,1)S(1)}, bf16[1,4,1,8,128]{4,1,3,2,0:T(4,128)(2,1)S(1)}, u32[]{:S(2)}, u32[]{:S(2)}) collective-permute-start(bf16[1,4,1,8,128]{4,1,3,2,0:T(4,128)(2,1)S(1)} %get-tuple-element.60), channel_id=1, source_target_pairs={{0,4},{4,8},{8,12},{1,5},{5,9},{9,13},{2,6},{6,10},{10,14},{3,7},{... | collective-permute-start | bytes 24584 | tf_op jit(solution)/shard_map/ppermute | solution.py:19
  12.9 5.5 %collective-permute-start.1 = (bf16[1,4,1,8,128]{4,1,3,2,0:T(4,128)(2,1)S(1)}, bf16[1,4,1,8,128]{4,1,3,2,0:T(4,128)(2,1)S(1)}, u32[]{:S(2)}, u32[]{:S(2)}) collective-permute-start(bf16[1,4,1,8,128]{4,1,3,2,0:T(4,128)(2,1)S(1)} %get-tuple-element.59), channel_id=1, source_target_pairs={{4,0},{8,4},{12,8},{5,1},{9,5},{13,9},{6,2},{10,6},{14,10},{7,3},{... | collective-permute-start | bytes 24584 | tf_op jit(solution)/shard_map/ppermute | solution.py:21
  14.2 15.8 %copy-start.46 = (bf16[1,4,1,8,128]{4,1,3,2,0:T(4,128)(2,1)}, bf16[1,4,1,8,128]{4,1,3,2,0:T(4,128)(2,1)S(1)}, u32[]{:S(2)}) copy-start(bf16[1,4,1,8,128]{4,1,3,2,0:T(4,128)(2,1)S(1)} %collective-permute-done) | copy-start | bytes 24580
  18.4 11.6 %copy-start.44 = (bf16[1,4,1,8,128]{4,1,3,2,0:T(4,128)(2,1)}, bf16[1,4,1,8,128]{4,1,3,2,0:T(4,128)(2,1)S(1)}, u32[]{:S(2)}) copy-start(bf16[1,4,1,8,128]{4,1,3,2,0:T(4,128)(2,1)S(1)} %collective-permute-done.1) | copy-start | bytes 24580
  18.4 42.6 %copy-start.28 = (bf16[1,4,4,8,128]{4,1,3,2,0:T(4,128)(2,1)}, bf16[1,4,4,8,128]{4,1,3,2,0:T(4,128)(2,1)S(1)}, u32[]{:S(2)}) copy-start(bf16[1,4,4,8,128]{4,1,3,2,0:T(4,128)(2,1)S(1)} %constant_dynamic-update-slice_fusion) | copy-start | bytes 98308
  18.5 11.4 %collective-permute-start.3 = (bf16[1,4,4,1,128]{4,1,3,2,0:T(4,128)(2,1)S(1)}, bf16[1,4,4,1,128]{4,1,3,2,0:T(4,128)(2,1)S(1)}, u32[]{:S(2)}, u32[]{:S(2)}) collective-permute-start(bf16[1,4,4,1,128]{4,1,3,2,0:T(4,128)(2,1)S(1)} %get-tuple-element.58), channel_id=1, source_target_pairs={{1,0},{2,1},{3,2},{5,4},{6,5},{7,6},{9,8},{10,9},{11,10},{13,12},{... | collective-permute-start | bytes 12296 | tf_op jit(solution)/shard_map/ppermute | solution.py:21
  19.8 10.1 %collective-permute-start.2 = (bf16[1,4,4,1,128]{4,1,3,2,0:T(4,128)(2,1)S(1)}, bf16[1,4,4,1,128]{4,1,3,2,0:T(4,128)(2,1)S(1)}, u32[]{:S(2)}, u32[]{:S(2)}) collective-permute-start(bf16[1,4,4,1,128]{4,1,3,2,0:T(4,128)(2,1)S(1)} %get-tuple-element.57), channel_id=1, source_target_pairs={{0,1},{1,2},{2,3},{4,5},{5,6},{6,7},{8,9},{9,10},{10,11},{12,13},{... | collective-permute-start | bytes 12296 | tf_op jit(solution)/shard_map/ppermute | solution.py:19
  28.8 3.1 copy-start.53
  28.8 3.1 copy-start.57
  29.9 31.2 %copy-start.42 = (bf16[1,4,4,1,128]{4,1,3,2,0:T(4,128)(2,1)}, bf16[1,4,4,1,128]{4,1,3,2,0:T(4,128)(2,1)S(1)}, u32[]{:S(2)}) copy-start(bf16[1,4,4,1,128]{4,1,3,2,0:T(4,128)(2,1)S(1)} %collective-permute-done.2) | copy-start | bytes 12292
  38.3 7.7 %copy-start.61 = (f32[2,8,8,17,32]{4,2,3,1,0:T(8,128)}, f32[2,8,8,17,32]{4,2,3,1,0:T(8,128)S(1)}, u32[]{:S(2)}) copy-start(f32[2,8,8,17,32]{4,2,3,1,0:T(8,128)S(1)} %fusion.38) | copy-start | bytes 835588
  46.5 14.6 %collective-permute-start.5 = (bf16[1,32,1,8,128]{4,1,3,2,0:T(8,128)(2,1)S(1)}, bf16[1,32,1,8,128]{4,1,3,2,0:T(8,128)(2,1)S(1)}, u32[]{:S(2)}, u32[]{:S(2)}) collective-permute-start(bf16[1,32,1,8,128]{4,1,3,2,0:T(8,128)(2,1)S(1)} %bitcast.753), channel_id=1, source_target_pairs={{4,0},{8,4},{12,8},{5,1},{9,5},{13,9},{6,2},{10,6},{14,10},{7,3},{... | collective-permute-start | bytes 196616 | tf_op jit(solution)/shard_map/ppermute | solution.py:21
  48.4 12.7 %collective-permute-start.4 = (bf16[1,32,1,8,128]{4,1,3,2,0:T(8,128)(2,1)S(1)}, bf16[1,32,1,8,128]{4,1,3,2,0:T(8,128)(2,1)S(1)}, u32[]{:S(2)}, u32[]{:S(2)}) collective-permute-start(bf16[1,32,1,8,128]{4,1,3,2,0:T(8,128)(2,1)S(1)} %bitcast.755), channel_id=1, source_target_pairs={{0,4},{4,8},{8,12},{1,5},{5,9},{9,13},{2,6},{6,10},{10,14},{3,7},{... | collective-permute-start | bytes 196616 | tf_op jit(solution)/shard_map/ppermute | solution.py:19
  53.6 13.4 %collective-permute-start.9 = (bf16[1,32,1,8,128]{4,1,3,2,0:T(8,128)(2,1)S(1)}, bf16[1,32,1,8,128]{4,1,3,2,0:T(8,128)(2,1)S(1)}, u32[]{:S(2)}, u32[]{:S(2)}) collective-permute-start(bf16[1,32,1,8,128]{4,1,3,2,0:T(8,128)(2,1)S(1)} %bitcast.754), channel_id=1, source_target_pairs={{4,0},{8,4},{12,8},{5,1},{9,5},{13,9},{6,2},{10,6},{14,10},{7,3},{... | collective-permute-start | bytes 196616 | tf_op jit(solution)/shard_map/ppermute | solution.py:21
  55.6 11.5 %collective-permute-start.8 = (bf16[1,32,1,8,128]{4,1,3,2,0:T(8,128)(2,1)S(1)}, bf16[1,32,1,8,128]{4,1,3,2,0:T(8,128)(2,1)S(1)}, u32[]{:S(2)}, u32[]{:S(2)}) collective-permute-start(bf16[1,32,1,8,128]{4,1,3,2,0:T(8,128)(2,1)S(1)} %bitcast.756), channel_id=1, source_target_pairs={{0,4},{4,8},{8,12},{1,5},{5,9},{9,13},{2,6},{6,10},{10,14},{3,7},{... | collective-permute-start | bytes 196616 | tf_op jit(solution)/shard_map/ppermute | solution.py:19
  61.1 12.5 %copy-start.3 = (bf16[1,32,1,8,128]{4,1,3,2,0:T(8,128)(2,1)}, bf16[1,32,1,8,128]{4,1,3,2,0:T(8,128)(2,1)S(1)}, u32[]{:S(2)}) copy-start(bf16[1,32,1,8,128]{4,1,3,2,0:T(8,128)(2,1)S(1)} %collective-permute-done.5) | copy-start | bytes 196612
  61.1 12.4 %copy-start.5 = (bf16[1,32,1,8,128]{4,1,3,2,0:T(8,128)(2,1)}, bf16[1,32,1,8,128]{4,1,3,2,0:T(8,128)(2,1)S(1)}, u32[]{:S(2)}) copy-start(bf16[1,32,1,8,128]{4,1,3,2,0:T(8,128)(2,1)S(1)} %collective-permute-done.4) | copy-start | bytes 196612
  61.2 12.4 %collective-permute-start.7 = (bf16[1,32,4,1,128]{4,1,3,2,0:T(8,128)(2,1)S(1)}, bf16[1,32,4,1,128]{4,1,3,2,0:T(8,128)(2,1)S(1)}, u32[]{:S(2)}, u32[]{:S(2)}) collective-permute-start(bf16[1,32,4,1,128]{4,1,3,2,0:T(8,128)(2,1)S(1)} %get-tuple-element.56), channel_id=1, source_target_pairs={{1,0},{2,1},{3,2},{5,4},{6,5},{7,6},{9,8},{10,9},{11,10},{13,12},{... | collective-permute-start | bytes 98312 | tf_op jit(solution)/shard_map/ppermute | solution.py:21
  62.5 11.1 %collective-permute-start.6 = (bf16[1,32,4,1,128]{4,1,3,2,0:T(8,128)(2,1)S(1)}, bf16[1,32,4,1,128]{4,1,3,2,0:T(8,128)(2,1)S(1)}, u32[]{:S(2)}, u32[]{:S(2)}) collective-permute-start(bf16[1,32,4,1,128]{4,1,3,2,0:T(8,128)(2,1)S(1)} %get-tuple-element.55), channel_id=1, source_target_pairs={{0,1},{1,2},{2,3},{4,5},{5,6},{6,7},{8,9},{9,10},{10,11},{12,13},{... | collective-permute-start | bytes 98312 | tf_op jit(solution)/shard_map/ppermute | solution.py:19
  67.0 6.6 %copy-start.7 = (bf16[1,32,1,8,128]{4,1,3,2,0:T(8,128)(2,1)}, bf16[1,32,1,8,128]{4,1,3,2,0:T(8,128)(2,1)S(1)}, u32[]{:S(2)}) copy-start(bf16[1,32,1,8,128]{4,1,3,2,0:T(8,128)(2,1)S(1)} %collective-permute-done.9) | copy-start | bytes 196612
  67.1 9.0 %copy-start.10 = (bf16[1,32,1,8,128]{4,1,3,2,0:T(8,128)(2,1)}, bf16[1,32,1,8,128]{4,1,3,2,0:T(8,128)(2,1)S(1)}, u32[]{:S(2)}) copy-start(bf16[1,32,1,8,128]{4,1,3,2,0:T(8,128)(2,1)S(1)} %collective-permute-done.8) | copy-start | bytes 196612
  67.7 8.4 %collective-permute-start.11 = (bf16[1,32,4,1,128]{4,1,3,2,0:T(8,128)(2,1)}, bf16[1,32,4,1,128]{4,1,3,2,0:T(8,128)(2,1)S(1)}, u32[]{:S(2)}, u32[]{:S(2)}) collective-permute-start(bf16[1,32,4,1,128]{4,1,3,2,0:T(8,128)(2,1)} %get-tuple-element.54), channel_id=1, source_target_pairs={{1,0},{2,1},{3,2},{5,4},{6,5},{7,6},{9,8},{10,9},{11,10},{13,12},{... | collective-permute-start | bytes 98312 | tf_op jit(solution)/shard_map/ppermute | solution.py:21
  69.0 7.1 %collective-permute-start.10 = (bf16[1,32,4,1,128]{4,1,3,2,0:T(8,128)(2,1)}, bf16[1,32,4,1,128]{4,1,3,2,0:T(8,128)(2,1)S(1)}, u32[]{:S(2)}, u32[]{:S(2)}) collective-permute-start(bf16[1,32,4,1,128]{4,1,3,2,0:T(8,128)(2,1)} %get-tuple-element.53), channel_id=1, source_target_pairs={{0,1},{1,2},{2,3},{4,5},{5,6},{6,7},{8,9},{9,10},{10,11},{12,13},{... | collective-permute-start | bytes 98312 | tf_op jit(solution)/shard_map/ppermute | solution.py:19
  82.6 41.7 %copy-start.55 = (f32[1,4]{1,0:T(1,128)S(1)}, f32[1,4]{1,0:T(1,128)}, u32[]{:S(2)}) copy-start(f32[1,4]{1,0:T(1,128)} %param.12) | copy-start | bytes 52
  82.6 41.7 %copy-start.56 = (f32[4]{0:T(128)S(1)}, f32[4]{0:T(128)}, u32[]{:S(2)}) copy-start(f32[4]{0:T(128)} %param.18) | copy-start | bytes 52
  82.6 42.0 %copy-start.48 = (f32[64,4]{0,1:T(4,128)S(1)}, f32[64,4]{0,1:T(4,128)}, u32[]{:S(2)}) copy-start(f32[64,4]{0,1:T(4,128)} %param.21) | copy-start | bytes 3076
  149.7 14.2 %collective-permute-start.13 = (bf16[2,1,64,1,8,128]{5,2,4,3,1,0:T(8,128)(2,1)S(1)}, bf16[2,1,64,1,8,128]{5,2,4,3,1,0:T(8,128)(2,1)S(1)}, u32[]{:S(2)}, u32[]{:S(2)}) collective-permute-start(bf16[2,1,64,1,8,128]{5,2,4,3,1,0:T(8,128)(2,1)S(1)} %get-tuple-element.48), channel_id=1, source_target_pairs={{4,0},{8,4},{12,8},{5,1},{9,5},{13,9},{6,2},{10,6},{14,10},{7,3},{... | collective-permute-start | bytes 786440 | tf_op jit(solution)/shard_map/ppermute | solution.py:21
  151.0 12.9 %collective-permute-start.12 = (bf16[2,1,64,1,8,128]{5,2,4,3,1,0:T(8,128)(2,1)S(1)}, bf16[2,1,64,1,8,128]{5,2,4,3,1,0:T(8,128)(2,1)S(1)}, u32[]{:S(2)}, u32[]{:S(2)}) collective-permute-start(bf16[2,1,64,1,8,128]{5,2,4,3,1,0:T(8,128)(2,1)S(1)} %get-tuple-element.47), channel_id=1, source_target_pairs={{0,4},{4,8},{8,12},{1,5},{5,9},{9,13},{2,6},{6,10},{10,14},{3,7},{... | collective-permute-start | bytes 786440 | tf_op jit(solution)/shard_map/ppermute | solution.py:19
  156.0 3.2 copy-start.36
  156.2 3.5 copy-start.34
  156.4 3.5 copy-start.40
  156.4 4.0 %copy-start.39 = (f32[64,32]{1,0:T(8,128)S(1)}, f32[64,32]{1,0:T(8,128)}, u32[]{:S(2)}) copy-start(f32[64,32]{1,0:T(8,128)} %convolution_bitcast_fusion.19) | copy-start | bytes 24580
  156.4 4.3 %copy-start.35 = (f32[64,32]{1,0:T(8,128)S(1)}, f32[64,32]{1,0:T(8,128)}, u32[]{:S(2)}) copy-start(f32[64,32]{1,0:T(8,128)} %convolution_bitcast_fusion.16) | copy-start | bytes 24580
  156.5 4.8 %copy-start.33 = (f32[64,32]{1,0:T(8,128)S(1)}, f32[64,32]{1,0:T(8,128)}, u32[]{:S(2)}) copy-start(f32[64,32]{1,0:T(8,128)} %convolution_bitcast_fusion.10) | copy-start | bytes 24580
  162.9 128.3 %copy-start.14 = (f32[27,2048]{1,0:T(8,128)S(1)}, f32[27,2048]{1,0:T(8,128)}, u32[]{:S(2)}) copy-start(f32[27,2048]{1,0:T(8,128)} %param.20) | copy-start | bytes 663556
  163.9 129.1 %collective-permute-start.15 = (bf16[2,1,64,4,1,128]{5,2,4,3,1,0:T(8,128)(2,1)S(1)}, bf16[2,1,64,4,1,128]{5,2,4,3,1,0:T(8,128)(2,1)S(1)}, u32[]{:S(2)}, u32[]{:S(2)}) collective-permute-start(bf16[2,1,64,4,1,128]{5,2,4,3,1,0:T(8,128)(2,1)S(1)} %get-tuple-element.42), channel_id=1, source_target_pairs={{1,0},{2,1},{3,2},{5,4},{6,5},{7,6},{9,8},{10,9},{11,10},{13,12},{... | collective-permute-start | bytes 393224 | tf_op jit(solution)/shard_map/ppermute | solution.py:21
  165.2 127.8 %collective-permute-start.14 = (bf16[2,1,64,4,1,128]{5,2,4,3,1,0:T(8,128)(2,1)S(1)}, bf16[2,1,64,4,1,128]{5,2,4,3,1,0:T(8,128)(2,1)S(1)}, u32[]{:S(2)}, u32[]{:S(2)}) collective-permute-start(bf16[2,1,64,4,1,128]{5,2,4,3,1,0:T(8,128)(2,1)S(1)} %get-tuple-element.41), channel_id=1, source_target_pairs={{0,1},{1,2},{2,3},{4,5},{5,6},{6,7},{8,9},{9,10},{10,11},{12,13},{... | collective-permute-start | bytes 393224 | tf_op jit(solution)/shard_map/ppermute | solution.py:19
  295.9 4.1 %copy-start.1 = (bf16[64,4,10,1,8,17]{0,4,5,2,1,3:T(8,128)(2,1)}, bf16[64,4,10,1,8,17]{0,4,5,2,1,3:T(8,128)(2,1)S(1)}, u32[]{:S(2)}) copy-start(bf16[64,4,10,1,8,17]{0,4,5,2,1,3:T(8,128)(2,1)S(1)} %copy.324) | copy-start | bytes 2088964
  310.9 3.0 copy-start.29
  310.9 3.0 copy-start.43
  311.3 3.0 copy-start.47
  312.3 3.6 copy-start.31
  313.2 4.1 %copy-start.45 = (bf16[1,4,1,8,128]{4,1,3,2,0:T(4,128)(2,1)S(1)}, bf16[1,4,1,8,128]{4,1,3,2,0:T(4,128)(2,1)}, u32[]{:S(2)}) copy-start(bf16[1,4,1,8,128]{4,1,3,2,0:T(4,128)(2,1)} %copy-done.44) | copy-start | bytes 24580
  314.0 43.8 %copy-start.32 = (f32[27,128]{1,0:T(8,128)S(1)}, f32[27,128]{1,0:T(8,128)}, u32[]{:S(2)}) copy-start(f32[27,128]{1,0:T(8,128)} %param.19) | copy-start | bytes 41476
  362.6 5.0 %copy-start.15 = (f32[27,2048]{1,0:T(8,128)S(1)}, f32[27,2048]{1,0:T(8,128)}, u32[]{:S(2)}) copy-start(f32[27,2048]{1,0:T(8,128)} %all-reduce.7.cloned.1.call-done) | copy-start | bytes 663556
  (33 other events, 48.0 us)
Sparse Core Ops, SparseCore 0:
  163.8 127.3 all-reduce.6
where the time goes:
time: 380 us; the launch traced here: 376 us
  waiting for transfers between devices  125 us (33%)
  blocking collectives  78.7 us (21%)
  matrix products  54.8 us (14%)
  starting transfers between devices  48.4 us (13%)
  local copies, waits for them, and re-layouts  35.4 us (9%)
  between operations  23.2 us (6%)
  other arithmetic  10.9 us (3%)
    psum x1, waiting for transfers between devices, per_device(): h1, h2, hd = lax.psum((h1, h2, hd), ('dp', 'gx', 'gy'))  122 us
    psum x1, blocking collectives, per_device(): h1, h2, hd = lax.psum((h1, h2, hd), ('dp', 'gx', 'gy'))  39.5 us
    psum x1, blocking collectives, per_device(): lax.psum((jnp.sum(act2, axis=(2, 3, 4)), jnp.sum(slope2 * t2, axis=(2, 3,...  39.3 us
    ppermute x8, starting transfers between devices, extended(): lax.ppermute(tail, axis, [(i, (i + 1) % count) for i in range(ends)])  38 us
    conv_general_dilated x8, matrix products, convolve(): lax.conv_general_dilated(pad_depth(padded), kernel, (1, 1, 1), 'VALID', d...  28.8 us
    dot_general x81, matrix products, correlate(): jnp.einsum('bixyz,boxyz->oi', window, grads, preferred_element_type=jnp.f...  25.3 us
    unnamed x145, local copies, waits for them, and re-layouts  13.8 us
    ppermute x8, starting transfers between devices, extended(): lax.ppermute(head, axis, [((i + 1) % count, i) for i in range(ends)])  10.3 us
  transfers between devices with their start and end apart: 17, of which 2 were waited for; matrix products, arithmetic and copies ran while one was open for 5% of the time, Pallas kernels for 0%

commit v1 on v0

--- a/solution.py
+++ b/solution.py
@@ -121,7 +121,7 @@
     tg1 = (bend1 * t1 * da1 + slope1 * tda1).astype(jnp.bfloat16)
     h1 = correlate(padded_in, tg1)
     h2 = correlate(pa1, tg2) + correlate(pta1, g2)
-    h1, h2, hd = lax.psum((h1, h2, hd), ("dp", "gx", "gy"))
+    h1, h2, hd = lax.psum(lax.psum((h1, h2, hd), ("gx", "gy")), "dp")
     field = tda1 * cells
     quad = jnp.sum(dir1 * h1) + jnp.sum(dir2 * h2) + jnp.sum(dir_head * hd)
     length = jnp.sum(dir1 * dir1) + jnp.sum(dir2 * dir2) + jnp.sum(dir_head * dir_head)

time: 380 us -> 401 us (1.055)
  blocking collectives: 78.7 us -> 118 us
  waiting for transfers between devices: 125 us -> 106 us
    psum x1 -> x2, blocking collectives: 39.5 us -> 78.6 us  [per_device(): h1, h2, hd = lax.psum(lax.psum((h1, h2, hd), ('gx', 'gy')), 'dp')]
    psum x1 -> x2, waiting for transfers between devices: 122 us -> 103 us  [per_device(): h1, h2, hd = lax.psum(lax.psum((h1, h2, hd), ('gx', 'gy')), 'dp')]
  transfers between devices with their start and end apart: 17 -> 18, of which waited for: 2 -> 2; matrix products, arithmetic and copies ran while one was open for 5% -> 11% of each run, Pallas kernels for 0% -> 0%
where the time goes in v1:
time: 401 us; the launch traced here: 397 us
  blocking collectives  118 us (29%)
  waiting for transfers between devices  106 us (26%)
  matrix products  54.8 us (14%)
  starting transfers between devices  48.4 us (12%)
  local copies, waits for them, and re-layouts  35.3 us (9%)
  between operations  23.1 us (6%)
  other arithmetic  11.4 us (3%)
    psum x2, waiting for transfers between devices, per_device(): h1, h2, hd = lax.psum(lax.psum((h1, h2, hd), ('gx', 'gy')), 'dp')  103 us
    psum x2, blocking collectives, per_device(): h1, h2, hd = lax.psum(lax.psum((h1, h2, hd), ('gx', 'gy')), 'dp')  78.6 us
    psum x1, blocking collectives, per_device(): lax.psum((jnp.sum(act2, axis=(2, 3, 4)), jnp.sum(slope2 * t2, axis=(2, 3,...  39.2 us
    ppermute x8, starting transfers between devices, extended(): lax.ppermute(tail, axis, [(i, (i + 1) % count) for i in range(ends)])  38 us
    conv_general_dilated x8, matrix products, convolve(): lax.conv_general_dilated(pad_depth(padded), kernel, (1, 1, 1), 'VALID', d...  28.8 us
    dot_general x81, matrix products, correlate(): jnp.einsum('bixyz,boxyz->oi', window, grads, preferred_element_type=jnp.f...  25.2 us
    unnamed x145, local copies, waits for them, and re-layouts  13.8 us
    ppermute x8, starting transfers between devices, extended(): lax.ppermute(head, axis, [((i + 1) % count, i) for i in range(ends)])  10.3 us
  transfers between devices with their start and end apart: 18, of which 2 were waited for; matrix products, arithmetic and copies ran while one was open for 11% of the time, Pallas kernels for 0%

profile of v1, /device:TPU:0, one launch (start us, length us, event | category | flops | bytes accessed | tf_op | source)
XLA Modules:
  0.0 397.2 jit_solution(15414566915685727354)
XLA Ops:
  8.0 4.9 %collective-permute-start = (bf16[1,4,1,8,128]{4,1,3,2,0:T(4,128)(2,1)S(1)}, bf16[1,4,1,8,128]{4,1,3,2,0:T(4,128)(2,1)S(1)}, u32[]{:S(2)}, u32[]{:S(2)}) collective-permute-start(bf16[1,4,1,8,128]{4,1,3,2,0:T(4,128)(2,1)S(1)} %get-tuple-element.62), channel_id=1, source_target_pairs={{0,4},{4,8},{8,12},{1,5},{5,9},{9,13},{2,6},{6,10},{10,14},{3,7},{... | collective-permute-start | bytes 24584 | tf_op jit(solution)/shard_map/ppermute | solution.py:19
  12.9 1.3 collective-permute-start.1
  15.0 3.5 collective-permute-done.1
  18.5 1.3 collective-permute-start.3
  19.8 4.5 %collective-permute-start.2 = (bf16[1,4,4,1,128]{4,1,3,2,0:T(4,128)(2,1)S(1)}, bf16[1,4,4,1,128]{4,1,3,2,0:T(4,128)(2,1)S(1)}, u32[]{:S(2)}, u32[]{:S(2)}) collective-permute-start(bf16[1,4,4,1,128]{4,1,3,2,0:T(4,128)(2,1)S(1)} %get-tuple-element.59), channel_id=1, source_target_pairs={{0,1},{1,2},{2,3},{4,5},{5,6},{6,7},{8,9},{9,10},{10,11},{12,13},{... | collective-permute-start | bytes 12296 | tf_op jit(solution)/shard_map/ppermute | solution.py:19
  24.3 2.0 reshape.567
  26.3 1.2 reshape.565
  28.8 1.1 reshape.570
  30.3 1.4 copy.299
  31.9 6.4 %fusion.38 = f32[2,8,8,17,32]{4,2,3,1,0:T(8,128)S(1)} fusion(bf16[3,3,3,32,4]{4,3,2,1,0:T(8,128)(2,1)S(1)} %reshape.565, f32[32]{0:T(128)S(1)} %copy-done.51, pred[8,17]{0,1:T(8,128)(4,1)S(1)} %copy-done.55, bf16[4,4,10,1,7,2]{4,0,5,2,1,3:T(4,128)(2,1)S(1)} %slice.473, bf16[4,4,10,1,8,17]{4,0,5,2,1,3:T(4,128)(2,1)S(1)} %copy.299), kind=kOutput, calls=%fused_computation.77 | convolution fusion | flops 15325696 | bytes 333704 | tf_op jit(solution)/shard_map/conv_general_dilated | solution.py:42
  38.3 7.7 %multiply_convert_fusion.1 = (bf16[2,8,8,17,32]{4,2,3,1,0:T(8,128)(2,1)S(1)}, bf16[2,8,8,17,32]{4,2,3,1,0:T(8,128)(2,1)S(1)}, f32[2,8,8,17,32]{4,2,3,1,0:T(8,128)}) fusion(f32[2,8,8,17,32]{4,2,3,1,0:T(8,128)S(1)} %fusion.38, bf16[3,3,3,32,4]{4,3,2,1,0:T(8,128)(2,1)S(1)} %reshape.566, bf16[4,4,10,1,7,2]{4,0,5,2,1,3:T(4,128)(2,1)S(1)} %slice.473, ...), kind=kOutput, calls=%fused_computation.95 | convolution fusion | flops 16022016 | bytes 890632 | tf_op jit(solution)/shard_map/conv_general_dilated | solution.py:42
  46.5 1.3 collective-permute-start.5
  48.4 4.9 %collective-permute-start.4 = (bf16[1,32,1,8,128]{4,1,3,2,0:T(8,128)(2,1)S(1)}, bf16[1,32,1,8,128]{4,1,3,2,0:T(8,128)(2,1)S(1)}, u32[]{:S(2)}, u32[]{:S(2)}) collective-permute-start(bf16[1,32,1,8,128]{4,1,3,2,0:T(8,128)(2,1)S(1)} %bitcast.755), channel_id=1, source_target_pairs={{0,4},{4,8},{8,12},{1,5},{5,9},{9,13},{2,6},{6,10},{10,14},{3,7},{... | collective-permute-start | bytes 196616 | tf_op jit(solution)/shard_map/ppermute | solution.py:19
  53.6 1.3 collective-permute-start.9
  55.6 5.4 %collective-permute-start.8 = (bf16[1,32,1,8,128]{4,1,3,2,0:T(8,128)(2,1)S(1)}, bf16[1,32,1,8,128]{4,1,3,2,0:T(8,128)(2,1)S(1)}, u32[]{:S(2)}, u32[]{:S(2)}) collective-permute-start(bf16[1,32,1,8,128]{4,1,3,2,0:T(8,128)(2,1)S(1)} %bitcast.756), channel_id=1, source_target_pairs={{0,4},{4,8},{8,12},{1,5},{5,9},{9,13},{2,6},{6,10},{10,14},{3,7},{... | collective-permute-start | bytes 196616 | tf_op jit(solution)/shard_map/ppermute | solution.py:19
  61.1 1.3 collective-permute-start.7
  62.4 4.5 %collective-permute-start.6 = (bf16[1,32,4,1,128]{4,1,3,2,0:T(8,128)(2,1)S(1)}, bf16[1,32,4,1,128]{4,1,3,2,0:T(8,128)(2,1)S(1)}, u32[]{:S(2)}, u32[]{:S(2)}) collective-permute-start(bf16[1,32,4,1,128]{4,1,3,2,0:T(8,128)(2,1)S(1)} %get-tuple-element.57), channel_id=1, source_target_pairs={{0,1},{1,2},{2,3},{4,5},{5,6},{6,7},{8,9},{9,10},{10,11},{12,13},{... | collective-permute-start | bytes 98312 | tf_op jit(solution)/shard_map/ppermute | solution.py:19
  67.7 1.3 collective-permute-start.11
  69.0 4.5 %collective-permute-start.10 = (bf16[1,32,4,1,128]{4,1,3,2,0:T(8,128)(2,1)}, bf16[1,32,4,1,128]{4,1,3,2,0:T(8,128)(2,1)S(1)}, u32[]{:S(2)}, u32[]{:S(2)}) collective-permute-start(bf16[1,32,4,1,128]{4,1,3,2,0:T(8,128)(2,1)} %get-tuple-element.55), channel_id=1, source_target_pairs={{0,1},{1,2},{2,3},{4,5},{5,6},{6,7},{8,9},{9,10},{10,11},{12,13},{... | collective-permute-start | bytes 98312 | tf_op jit(solution)/shard_map/ppermute | solution.py:19
  78.7 1.9 convolution_select_fusion.2
  80.7 1.9 fusion.37
  82.6 2.4 select_reduce_fusion
  85.1 39.2 %all-reduce.4 = (f32[1,64]{1,0:T(1,128)S(1)}, f32[1,64]{1,0:T(1,128)S(1)}) all-reduce(f32[1,64]{1,0:T(1,128)S(1)} %bitcast.760, f32[1,64]{1,0:T(1,128)S(1)} %bitcast.759), channel_id=1, replica_groups=mesh['dp'=2,'gx'=4,'gy'=4] {'gx','gy'}, use_global_device_ids=true, to_apply=%region_1.2 | all-reduce | flops 128 | bytes 1024 | tf_op jit(solution)/shard_map/psum | solution.py:97
  125.7 2.1 multiply_convert_fusion
  130.9 0.8 convolution_bitcast_fusion.52
  131.7 0.8 convolution_bitcast_fusion.43
  133.9 0.8 convolution_bitcast_fusion.46
  136.1 0.8 convolution_bitcast_fusion.34
  138.1 0.8 convolution_bitcast_fusion.28
  142.3 0.8 convolution_bitcast_fusion.25
  143.1 0.8 convolution_bitcast_fusion.16
  145.3 0.8 convolution_bitcast_fusion.19
  149.1 1.3 collective-permute-start.13
  150.4 4.6 %collective-permute-start.12 = (bf16[2,1,64,1,8,128]{5,2,4,3,1,0:T(8,128)(2,1)S(1)}, bf16[2,1,64,1,8,128]{5,2,4,3,1,0:T(8,128)(2,1)S(1)}, u32[]{:S(2)}, u32[]{:S(2)}) collective-permute-start(bf16[2,1,64,1,8,128]{5,2,4,3,1,0:T(8,128)(2,1)S(1)} %get-tuple-element.49), channel_id=1, source_target_pairs={{0,4},{4,8},{8,12},{1,5},{5,9},{9,13},{2,6},{6,10},{10,14},{3,7},{... | collective-permute-start | bytes 786440 | tf_op jit(solution)/shard_map/ppermute | solution.py:19
  156.3 0.8 stack.293
  163.3 1.3 collective-permute-start.15
  164.6 4.6 %collective-permute-start.14 = (bf16[2,1,64,4,1,128]{5,2,4,3,1,0:T(8,128)(2,1)S(1)}, bf16[2,1,64,4,1,128]{5,2,4,3,1,0:T(8,128)(2,1)S(1)}, u32[]{:S(2)}, u32[]{:S(2)}) collective-permute-start(bf16[2,1,64,4,1,128]{5,2,4,3,1,0:T(8,128)(2,1)S(1)} %get-tuple-element.43), channel_id=1, source_target_pairs={{0,1},{1,2},{2,3},{4,5},{5,6},{6,7},{8,9},{9,10},{10,11},{12,13},{... | collective-permute-start | bytes 393224 | tf_op jit(solution)/shard_map/ppermute | solution.py:19
  169.3 102.6 %all-reduce.9.cloned.1.call-done = f32[27,2048]{1,0:T(8,128)} async-done(((f32[27,2048]{1,0:T(8,128)}), f32[27,2048]{1,0:T(8,128)}) %all-reduce.9.cloned.1.call-update) | async-done | bytes 221200 | tf_op jit(solution)/shard_map/psum | solution.py:124
  272.3 1.6 copy.591
  275.6 3.3 convolution_select_fusion
  278.9 1.8 copy.592
  282.8 2.4 broadcast_multiply_fusion
  285.3 2.7 fusion.39
  297.5 1.1 copy.415
  298.7 75.2 %all-reduce.3 = (f32[27,128]{1,0:T(8,128)S(1)}, f32[64,4]{0,1:T(4,128)S(1)}) all-reduce(f32[27,128]{1,0:T(8,128)S(1)} %stack.291, f32[64,4]{0,1:T(4,128)S(1)} %add_multiply_fusion), channel_id=1, replica_groups=mesh['dp'=2,'gx'=4,'gy'=4] {'gx','gy'}, use_global_device_ids=true, to_apply=%region_4.5 | all-reduce | flops 3712 | bytes 29696 | tf_op jit(solution)/shard_map/psum | solution.py:124
  373.9 3.4 all-reduce.5
  378.6 1.7 multiply_reduce_fusion
  387.3 1.7 broadcast_divide_fusion
  (388 shorter events, 50.1 us)
Async XLA Ops:
  7.2 117.2 %copy-start = (f32[64,4]{0,1:T(4,128)S(1)}, f32[64,4]{0,1:T(4,128)}, u32[]{:S(2)}) copy-start(f32[64,4]{0,1:T(4,128)} %param.17) | copy-start | bytes 3076
  7.2 21.5 %copy-start.13 = (f32[27,2048]{1,0:T(8,128)S(1)}, f32[27,2048]{1,0:T(8,128)}, u32[]{:S(2)}) copy-start(f32[27,2048]{1,0:T(8,128)} %param.20) | copy-start | bytes 663556
  7.2 264.7 %all-reduce.9.cloned.1.call-start = ((), (), s32[]{:S(2)}) async-start(), calls=%async_computation | async-start | bytes 524288 | tf_op jit(solution)/shard_map/psum | solution.py:124
  8.0 6.2 %collective-permute-start = (bf16[1,4,1,8,128]{4,1,3,2,0:T(4,128)(2,1)S(1)}, bf16[1,4,1,8,128]{4,1,3,2,0:T(4,128)(2,1)S(1)}, u32[]{:S(2)}, u32[]{:S(2)}) collective-permute-start(bf16[1,4,1,8,128]{4,1,3,2,0:T(4,128)(2,1)S(1)} %get-tuple-element.62), channel_id=1, source_target_pairs={{0,4},{4,8},{8,12},{1,5},{5,9},{9,13},{2,6},{6,10},{10,14},{3,7},{... | collective-permute-start | bytes 24584 | tf_op jit(solution)/shard_map/ppermute | solution.py:19
  12.9 5.5 %collective-permute-start.1 = (bf16[1,4,1,8,128]{4,1,3,2,0:T(4,128)(2,1)S(1)}, bf16[1,4,1,8,128]{4,1,3,2,0:T(4,128)(2,1)S(1)}, u32[]{:S(2)}, u32[]{:S(2)}) collective-permute-start(bf16[1,4,1,8,128]{4,1,3,2,0:T(4,128)(2,1)S(1)} %get-tuple-element.61), channel_id=1, source_target_pairs={{4,0},{8,4},{12,8},{5,1},{9,5},{13,9},{6,2},{10,6},{14,10},{7,3},{... | collective-permute-start | bytes 24584 | tf_op jit(solution)/shard_map/ppermute | solution.py:21
  14.2 15.8 %copy-start.45 = (bf16[1,4,1,8,128]{4,1,3,2,0:T(4,128)(2,1)}, bf16[1,4,1,8,128]{4,1,3,2,0:T(4,128)(2,1)S(1)}, u32[]{:S(2)}) copy-start(bf16[1,4,1,8,128]{4,1,3,2,0:T(4,128)(2,1)S(1)} %collective-permute-done) | copy-start | bytes 24580
  18.4 11.6 %copy-start.43 = (bf16[1,4,1,8,128]{4,1,3,2,0:T(4,128)(2,1)}, bf16[1,4,1,8,128]{4,1,3,2,0:T(4,128)(2,1)S(1)}, u32[]{:S(2)}) copy-start(bf16[1,4,1,8,128]{4,1,3,2,0:T(4,128)(2,1)S(1)} %collective-permute-done.1) | copy-start | bytes 24580
  18.4 42.6 %copy-start.27 = (bf16[1,4,4,8,128]{4,1,3,2,0:T(4,128)(2,1)}, bf16[1,4,4,8,128]{4,1,3,2,0:T(4,128)(2,1)S(1)}, u32[]{:S(2)}) copy-start(bf16[1,4,4,8,128]{4,1,3,2,0:T(4,128)(2,1)S(1)} %constant_dynamic-update-slice_fusion) | copy-start | bytes 98308
  18.5 11.4 %collective-permute-start.3 = (bf16[1,4,4,1,128]{4,1,3,2,0:T(4,128)(2,1)S(1)}, bf16[1,4,4,1,128]{4,1,3,2,0:T(4,128)(2,1)S(1)}, u32[]{:S(2)}, u32[]{:S(2)}) collective-permute-start(bf16[1,4,4,1,128]{4,1,3,2,0:T(4,128)(2,1)S(1)} %get-tuple-element.60), channel_id=1, source_target_pairs={{1,0},{2,1},{3,2},{5,4},{6,5},{7,6},{9,8},{10,9},{11,10},{13,12},{... | collective-permute-start | bytes 12296 | tf_op jit(solution)/shard_map/ppermute | solution.py:21
  19.8 10.1 %collective-permute-start.2 = (bf16[1,4,4,1,128]{4,1,3,2,0:T(4,128)(2,1)S(1)}, bf16[1,4,4,1,128]{4,1,3,2,0:T(4,128)(2,1)S(1)}, u32[]{:S(2)}, u32[]{:S(2)}) collective-permute-start(bf16[1,4,4,1,128]{4,1,3,2,0:T(4,128)(2,1)S(1)} %get-tuple-element.59), channel_id=1, source_target_pairs={{0,1},{1,2},{2,3},{4,5},{5,6},{6,7},{8,9},{9,10},{10,11},{12,13},{... | collective-permute-start | bytes 12296 | tf_op jit(solution)/shard_map/ppermute | solution.py:19
  28.8 3.1 copy-start.51
  28.8 3.1 copy-start.55
  29.9 31.2 %copy-start.41 = (bf16[1,4,4,1,128]{4,1,3,2,0:T(4,128)(2,1)}, bf16[1,4,4,1,128]{4,1,3,2,0:T(4,128)(2,1)S(1)}, u32[]{:S(2)}) copy-start(bf16[1,4,4,1,128]{4,1,3,2,0:T(4,128)(2,1)S(1)} %collective-permute-done.2) | copy-start | bytes 12292
  38.3 7.7 %copy-start.61 = (f32[2,8,8,17,32]{4,2,3,1,0:T(8,128)}, f32[2,8,8,17,32]{4,2,3,1,0:T(8,128)S(1)}, u32[]{:S(2)}) copy-start(f32[2,8,8,17,32]{4,2,3,1,0:T(8,128)S(1)} %fusion.38) | copy-start | bytes 835588
  46.5 14.6 %collective-permute-start.5 = (bf16[1,32,1,8,128]{4,1,3,2,0:T(8,128)(2,1)S(1)}, bf16[1,32,1,8,128]{4,1,3,2,0:T(8,128)(2,1)S(1)}, u32[]{:S(2)}, u32[]{:S(2)}) collective-permute-start(bf16[1,32,1,8,128]{4,1,3,2,0:T(8,128)(2,1)S(1)} %bitcast.753), channel_id=1, source_target_pairs={{4,0},{8,4},{12,8},{5,1},{9,5},{13,9},{6,2},{10,6},{14,10},{7,3},{... | collective-permute-start | bytes 196616 | tf_op jit(solution)/shard_map/ppermute | solution.py:21
  48.4 12.7 %collective-permute-start.4 = (bf16[1,32,1,8,128]{4,1,3,2,0:T(8,128)(2,1)S(1)}, bf16[1,32,1,8,128]{4,1,3,2,0:T(8,128)(2,1)S(1)}, u32[]{:S(2)}, u32[]{:S(2)}) collective-permute-start(bf16[1,32,1,8,128]{4,1,3,2,0:T(8,128)(2,1)S(1)} %bitcast.755), channel_id=1, source_target_pairs={{0,4},{4,8},{8,12},{1,5},{5,9},{9,13},{2,6},{6,10},{10,14},{3,7},{... | collective-permute-start | bytes 196616 | tf_op jit(solution)/shard_map/ppermute | solution.py:19
  53.6 13.4 %collective-permute-start.9 = (bf16[1,32,1,8,128]{4,1,3,2,0:T(8,128)(2,1)S(1)}, bf16[1,32,1,8,128]{4,1,3,2,0:T(8,128)(2,1)S(1)}, u32[]{:S(2)}, u32[]{:S(2)}) collective-permute-start(bf16[1,32,1,8,128]{4,1,3,2,0:T(8,128)(2,1)S(1)} %bitcast.754), channel_id=1, source_target_pairs={{4,0},{8,4},{12,8},{5,1},{9,5},{13,9},{6,2},{10,6},{14,10},{7,3},{... | collective-permute-start | bytes 196616 | tf_op jit(solution)/shard_map/ppermute | solution.py:21
  55.6 11.5 %collective-permute-start.8 = (bf16[1,32,1,8,128]{4,1,3,2,0:T(8,128)(2,1)S(1)}, bf16[1,32,1,8,128]{4,1,3,2,0:T(8,128)(2,1)S(1)}, u32[]{:S(2)}, u32[]{:S(2)}) collective-permute-start(bf16[1,32,1,8,128]{4,1,3,2,0:T(8,128)(2,1)S(1)} %bitcast.756), channel_id=1, source_target_pairs={{0,4},{4,8},{8,12},{1,5},{5,9},{9,13},{2,6},{6,10},{10,14},{3,7},{... | collective-permute-start | bytes 196616 | tf_op jit(solution)/shard_map/ppermute | solution.py:19
  61.1 12.5 %copy-start.3 = (bf16[1,32,1,8,128]{4,1,3,2,0:T(8,128)(2,1)}, bf16[1,32,1,8,128]{4,1,3,2,0:T(8,128)(2,1)S(1)}, u32[]{:S(2)}) copy-start(bf16[1,32,1,8,128]{4,1,3,2,0:T(8,128)(2,1)S(1)} %collective-permute-done.5) | copy-start | bytes 196612
  61.1 12.5 %copy-start.5 = (bf16[1,32,1,8,128]{4,1,3,2,0:T(8,128)(2,1)}, bf16[1,32,1,8,128]{4,1,3,2,0:T(8,128)(2,1)S(1)}, u32[]{:S(2)}) copy-start(bf16[1,32,1,8,128]{4,1,3,2,0:T(8,128)(2,1)S(1)} %collective-permute-done.4) | copy-start | bytes 196612
  61.1 12.4 %collective-permute-start.7 = (bf16[1,32,4,1,128]{4,1,3,2,0:T(8,128)(2,1)S(1)}, bf16[1,32,4,1,128]{4,1,3,2,0:T(8,128)(2,1)S(1)}, u32[]{:S(2)}, u32[]{:S(2)}) collective-permute-start(bf16[1,32,4,1,128]{4,1,3,2,0:T(8,128)(2,1)S(1)} %get-tuple-element.58), channel_id=1, source_target_pairs={{1,0},{2,1},{3,2},{5,4},{6,5},{7,6},{9,8},{10,9},{11,10},{13,12},{... | collective-permute-start | bytes 98312 | tf_op jit(solution)/shard_map/ppermute | solution.py:21
  62.4 11.1 %collective-permute-start.6 = (bf16[1,32,4,1,128]{4,1,3,2,0:T(8,128)(2,1)S(1)}, bf16[1,32,4,1,128]{4,1,3,2,0:T(8,128)(2,1)S(1)}, u32[]{:S(2)}, u32[]{:S(2)}) collective-permute-start(bf16[1,32,4,1,128]{4,1,3,2,0:T(8,128)(2,1)S(1)} %get-tuple-element.57), channel_id=1, source_target_pairs={{0,1},{1,2},{2,3},{4,5},{5,6},{6,7},{8,9},{9,10},{10,11},{12,13},{... | collective-permute-start | bytes 98312 | tf_op jit(solution)/shard_map/ppermute | solution.py:19
  67.0 6.6 %copy-start.7 = (bf16[1,32,1,8,128]{4,1,3,2,0:T(8,128)(2,1)}, bf16[1,32,1,8,128]{4,1,3,2,0:T(8,128)(2,1)S(1)}, u32[]{:S(2)}) copy-start(bf16[1,32,1,8,128]{4,1,3,2,0:T(8,128)(2,1)S(1)} %collective-permute-done.9) | copy-start | bytes 196612
  67.0 9.0 %copy-start.10 = (bf16[1,32,1,8,128]{4,1,3,2,0:T(8,128)(2,1)}, bf16[1,32,1,8,128]{4,1,3,2,0:T(8,128)(2,1)S(1)}, u32[]{:S(2)}) copy-start(bf16[1,32,1,8,128]{4,1,3,2,0:T(8,128)(2,1)S(1)} %collective-permute-done.8) | copy-start | bytes 196612
  67.7 8.4 %collective-permute-start.11 = (bf16[1,32,4,1,128]{4,1,3,2,0:T(8,128)(2,1)}, bf16[1,32,4,1,128]{4,1,3,2,0:T(8,128)(2,1)S(1)}, u32[]{:S(2)}, u32[]{:S(2)}) collective-permute-start(bf16[1,32,4,1,128]{4,1,3,2,0:T(8,128)(2,1)} %get-tuple-element.56), channel_id=1, source_target_pairs={{1,0},{2,1},{3,2},{5,4},{6,5},{7,6},{9,8},{10,9},{11,10},{13,12},{... | collective-permute-start | bytes 98312 | tf_op jit(solution)/shard_map/ppermute | solution.py:21
  69.0 7.1 %collective-permute-start.10 = (bf16[1,32,4,1,128]{4,1,3,2,0:T(8,128)(2,1)}, bf16[1,32,4,1,128]{4,1,3,2,0:T(8,128)(2,1)S(1)}, u32[]{:S(2)}, u32[]{:S(2)}) collective-permute-start(bf16[1,32,4,1,128]{4,1,3,2,0:T(8,128)(2,1)} %get-tuple-element.55), channel_id=1, source_target_pairs={{0,1},{1,2},{2,3},{4,5},{5,6},{6,7},{8,9},{9,10},{10,11},{12,13},{... | collective-permute-start | bytes 98312 | tf_op jit(solution)/shard_map/ppermute | solution.py:19
  82.6 41.7 %copy-start.53 = (f32[1,4]{1,0:T(1,128)S(1)}, f32[1,4]{1,0:T(1,128)}, u32[]{:S(2)}) copy-start(f32[1,4]{1,0:T(1,128)} %param.12) | copy-start | bytes 52
  82.6 41.7 %copy-start.54 = (f32[4]{0:T(128)S(1)}, f32[4]{0:T(128)}, u32[]{:S(2)}) copy-start(f32[4]{0:T(128)} %param.18) | copy-start | bytes 52
  82.6 42.0 %copy-start.47 = (f32[64,4]{0,1:T(4,128)S(1)}, f32[64,4]{0,1:T(4,128)}, u32[]{:S(2)}) copy-start(f32[64,4]{0,1:T(4,128)} %param.21) | copy-start | bytes 3076
  124.3 3.4 copy-start.58
  149.1 14.1 %collective-permute-start.13 = (bf16[2,1,64,1,8,128]{5,2,4,3,1,0:T(8,128)(2,1)S(1)}, bf16[2,1,64,1,8,128]{5,2,4,3,1,0:T(8,128)(2,1)S(1)}, u32[]{:S(2)}, u32[]{:S(2)}) collective-permute-start(bf16[2,1,64,1,8,128]{5,2,4,3,1,0:T(8,128)(2,1)S(1)} %get-tuple-element.50), channel_id=1, source_target_pairs={{4,0},{8,4},{12,8},{5,1},{9,5},{13,9},{6,2},{10,6},{14,10},{7,3},{... | collective-permute-start | bytes 786440 | tf_op jit(solution)/shard_map/ppermute | solution.py:21
  150.4 12.8 %collective-permute-start.12 = (bf16[2,1,64,1,8,128]{5,2,4,3,1,0:T(8,128)(2,1)S(1)}, bf16[2,1,64,1,8,128]{5,2,4,3,1,0:T(8,128)(2,1)S(1)}, u32[]{:S(2)}, u32[]{:S(2)}) collective-permute-start(bf16[2,1,64,1,8,128]{5,2,4,3,1,0:T(8,128)(2,1)S(1)} %get-tuple-element.49), channel_id=1, source_target_pairs={{0,4},{4,8},{8,12},{1,5},{5,9},{9,13},{2,6},{6,10},{10,14},{3,7},{... | collective-permute-start | bytes 786440 | tf_op jit(solution)/shard_map/ppermute | solution.py:19
  155.4 3.2 copy-start.35
  155.7 3.5 copy-start.33
  155.9 3.5 copy-start.39
  155.9 4.0 %copy-start.38 = (f32[64,32]{1,0:T(8,128)S(1)}, f32[64,32]{1,0:T(8,128)}, u32[]{:S(2)}) copy-start(f32[64,32]{1,0:T(8,128)} %convolution_bitcast_fusion.19) | copy-start | bytes 24580
  155.9 4.3 %copy-start.34 = (f32[64,32]{1,0:T(8,128)S(1)}, f32[64,32]{1,0:T(8,128)}, u32[]{:S(2)}) copy-start(f32[64,32]{1,0:T(8,128)} %convolution_bitcast_fusion.16) | copy-start | bytes 24580
  155.9 4.8 %copy-start.32 = (f32[64,32]{1,0:T(8,128)S(1)}, f32[64,32]{1,0:T(8,128)}, u32[]{:S(2)}) copy-start(f32[64,32]{1,0:T(8,128)} %convolution_bitcast_fusion.10) | copy-start | bytes 24580
  162.4 6.8 %copy-start.48 = (f32[64]{0:T(128)S(1)}, f32[64]{0:T(128)}, u32[]{:S(2)}) copy-start(f32[64]{0:T(128)} %fusion.305) | copy-start | bytes 772
  162.4 6.8 %copy-start.50 = (f32[4]{0:T(128)S(1)}, f32[4]{0:T(128)}, u32[]{:S(2)}) copy-start(f32[4]{0:T(128)} %copy-done.49) | copy-start | bytes 52
  163.2 215.5 %all-reduce.11.cloned.1.call-start = ((), (), s32[]{:S(2)}) async-start(), calls=%async_computation.1 | async-start | bytes 524288 | tf_op jit(solution)/shard_map/psum | solution.py:124
  163.3 108.6 %collective-permute-start.15 = (bf16[2,1,64,4,1,128]{5,2,4,3,1,0:T(8,128)(2,1)S(1)}, bf16[2,1,64,4,1,128]{5,2,4,3,1,0:T(8,128)(2,1)S(1)}, u32[]{:S(2)}, u32[]{:S(2)}) collective-permute-start(bf16[2,1,64,4,1,128]{5,2,4,3,1,0:T(8,128)(2,1)S(1)} %get-tuple-element.44), channel_id=1, source_target_pairs={{1,0},{2,1},{3,2},{5,4},{6,5},{7,6},{9,8},{10,9},{11,10},{13,12},{... | collective-permute-start | bytes 393224 | tf_op jit(solution)/shard_map/ppermute | solution.py:21
  164.6 107.3 %collective-permute-start.14 = (bf16[2,1,64,4,1,128]{5,2,4,3,1,0:T(8,128)(2,1)S(1)}, bf16[2,1,64,4,1,128]{5,2,4,3,1,0:T(8,128)(2,1)S(1)}, u32[]{:S(2)}, u32[]{:S(2)}) collective-permute-start(bf16[2,1,64,4,1,128]{5,2,4,3,1,0:T(8,128)(2,1)S(1)} %get-tuple-element.43), channel_id=1, source_target_pairs={{0,1},{1,2},{2,3},{4,5},{5,6},{6,7},{8,9},{9,10},{10,11},{12,13},{... | collective-permute-start | bytes 393224 | tf_op jit(solution)/shard_map/ppermute | solution.py:19
  274.8 4.1 %copy-start.1 = (bf16[64,4,10,1,8,17]{0,4,5,2,1,3:T(8,128)(2,1)}, bf16[64,4,10,1,8,17]{0,4,5,2,1,3:T(8,128)(2,1)S(1)}, u32[]{:S(2)}) copy-start(bf16[64,4,10,1,8,17]{0,4,5,2,1,3:T(8,128)(2,1)S(1)} %copy.324) | copy-start | bytes 2088964
  291.2 3.6 copy-start.30
  292.2 4.1 %copy-start.44 = (bf16[1,4,1,8,128]{4,1,3,2,0:T(4,128)(2,1)S(1)}, bf16[1,4,1,8,128]{4,1,3,2,0:T(4,128)(2,1)}, u32[]{:S(2)}) copy-start(bf16[1,4,1,8,128]{4,1,3,2,0:T(4,128)(2,1)} %copy-done.43) | copy-start | bytes 24580
  297.5 80.5 %copy-start.31 = (f32[27,128]{1,0:T(8,128)S(1)}, f32[27,128]{1,0:T(8,128)}, u32[]{:S(2)}) copy-start(f32[27,128]{1,0:T(8,128)} %param.19) | copy-start | bytes 41476
  297.5 81.1 %copy-start.14 = (f32[27,2048]{1,0:T(8,128)S(1)}, f32[27,2048]{1,0:T(8,128)}, u32[]{:S(2)}) copy-start(f32[27,2048]{1,0:T(8,128)} %param.20) | copy-start | bytes 663556
  (34 other events, 53.1 us)
Sparse Core Ops, SparseCore 0:
  163.3 108.5 all-reduce.8
  274.2 17.2 all-reduce.10
